TPU v7x, 32 devices: a whole 2x2x4 slice. The times are simulated.
32 devices in a mesh: rep: 8 (over z, x), tp: 4 (over y, core).
Axes of the slice: x: 2, y: 2, z: 4, core: 2. Of those that a mesh axis runs over, the one named last changes fastest.
Arguments:
- stream_in: bfloat16 [32, 4, 8192], P('rep', None, 'tp'), may hold values from -6 to 6
- queries: bfloat16 [32, 4, 4096], P('rep'), may hold values from -90 to 90
- new_keys: bfloat16 [32, 4, 4, 128], P('rep'), may hold values from -4 to 4
- new_values: bfloat16 [32, 4, 4, 128], P('rep'), may hold values from -4 to 4
- key_cache: bfloat16 [32, 1024, 4, 128], P('rep', 'tp'), may hold values from -4.1 to 4.1
- value_cache: bfloat16 [32, 1024, 4, 128], P('rep', 'tp'), may hold values from -4 to 4
- lengths: int32 [32], P('rep'), may hold values from 2 to 1024
- out_weight: bfloat16 [4096, 8192], P('tp', 'rep'), may hold values from -0.09375 to 0.09375
- norm_gain: bfloat16 [8192], P('tp'), may hold values from 0.5 to 1.5
Outputs:
- stream_out: bfloat16 [32, 4, 8192], P('rep', None, 'tp')
- normed: bfloat16 [32, 4, 8192], P('rep', None, 'tp')
All inputs are finite; a program needn't handle non-finite values.
Results may differ from a plain program's by a relative error of at most 0.0065.
Values may be sent and summed in bfloat16 or wider, within the bound.
A program may use at most 64 MiB of HBM per device.

v0:
```python
import math
import jax
import jax.numpy as jnp
from jax import lax
from jax.sharding import PartitionSpec as P

D = 8192


def on_device(
    stream_in, queries, new_keys, new_values, key_cache, value_cache, lengths, out_weight, norm_gain
):
    row_count, step_count, width = queries.shape
    kv_heads, head_dim = (key_cache.shape[2], key_cache.shape[3])
    block_len = key_cache.shape[1]
    group_size = width // head_dim // kv_heads
    tp_index = lax.axis_index("tp")
    scaling = 1.0 / math.sqrt(head_dim)
    grouped = queries.reshape(row_count, step_count, kv_heads, group_size, head_dim)
    cached = (
        jnp.einsum("bsgjd,bpgd->bsgjp", grouped, key_cache, preferred_element_type=jnp.float32)
        * scaling
    )
    positions = tp_index * block_len + jnp.arange(block_len, dtype=jnp.int32)
    visible = positions[None, :] < lengths[:, None]
    cached = jnp.where(visible[:, None, None, None, :], cached, -1e30)
    fresh = (
        jnp.einsum("bsgjd,btgd->bsgjt", grouped, new_keys, preferred_element_type=jnp.float32)
        * scaling
    )
    causal = (jnp.arange(step_count)[None, :] <= jnp.arange(step_count)[:, None]) & (tp_index == 0)
    fresh = jnp.where(causal[None, :, None, None, :], fresh, -1e30)
    local_maxima = jnp.maximum(cached.max(-1), fresh.max(-1))
    maxima = lax.pmax(local_maxima, "tp")
    weights_cached = jnp.exp(cached - maxima[..., None])
    weights_fresh = jnp.exp(fresh - maxima[..., None])
    denominator = weights_cached.sum(-1) + weights_fresh.sum(-1)
    numerator = jnp.einsum(
        "bsgjp,bpgd->bsgjd",
        weights_cached.astype(jnp.bfloat16),
        value_cache,
        preferred_element_type=jnp.float32,
    )
    numerator = numerator + jnp.einsum(
        "bsgjt,btgd->bsgjd",
        weights_fresh.astype(jnp.bfloat16),
        new_values,
        preferred_element_type=jnp.float32,
    )
    numerator = numerator.reshape(row_count, step_count, kv_heads * group_size, head_dim)
    denominator = denominator.reshape(row_count, step_count, kv_heads * group_size)
    numerator, denominator = (
        lax.psum_scatter(
            numerator.astype(jnp.bfloat16), "tp", scatter_dimension=2, tiled=True
        ).astype(jnp.float32),
        lax.psum_scatter(
            denominator.astype(jnp.bfloat16), "tp", scatter_dimension=2, tiled=True
        ).astype(jnp.float32),
    )
    attended = (numerator / denominator[..., None]).astype(jnp.bfloat16)
    attended = attended.reshape(row_count * step_count, -1)
    projected = jnp.dot(
        lax.all_gather(attended, "rep", axis=0, tiled=True),
        out_weight,
        preferred_element_type=jnp.float32,
    ).astype(jnp.bfloat16)
    partial_value = lax.all_to_all(
        projected, "rep", split_axis=0, concat_axis=1, tiled=True
    ).astype(jnp.float32)
    summed = lax.psum_scatter(
        partial_value.astype(jnp.bfloat16), "tp", scatter_dimension=1, tiled=True
    ).astype(jnp.float32)
    hidden = stream_in.reshape(row_count * step_count, -1).astype(jnp.float32) + summed
    squares = lax.psum(jnp.sum(hidden * hidden, axis=1), "tp")
    inverse = lax.rsqrt(squares / D + 1e-06)
    normed = hidden * inverse[:, None] * norm_gain.astype(jnp.float32)[None, :]
    stream_out = hidden.astype(jnp.bfloat16).reshape(row_count, step_count, -1)
    return (stream_out, normed.astype(jnp.bfloat16).reshape(row_count, step_count, -1))


def solution(mesh):
    return jax.shard_map(
        on_device,
        mesh=mesh,
        in_specs=(
            P("rep", None, "tp"),
            P("rep", None, None),
            P("rep", None, None, None),
            P("rep", None, None, None),
            P("rep", "tp", None, None),
            P("rep", "tp", None, None),
            P("rep"),
            P("tp", "rep"),
            P("tp"),
        ),
        out_specs=(P("rep", None, "tp"), P("rep", None, "tp")),
        check_vma=False,
    )
```

profile of v0, /device:TPU:0, one launch (start us, length us, event | category | flops | bytes accessed | tf_op | source)
XLA Modules:
  0.0 127.4 jit_solution(1407445413883382145)
XLA Ops:
  7.2 0.0 copy-start
  7.2 0.0 copy-start.4
  7.2 0.0 reduce-scatter.8.cloned.1.call-start
  7.2 1.2 reshape.73
  8.5 0.7 broadcast_compare_fusion
  9.2 0.0 copy-start.2
  9.2 1.8 %fusion.23 = (f32[4,4,4,8]{3,1,2,0:T(4,128)S(1)}, f32[4,4,4,8,256]{4,3,1,2,0:T(8,128)S(1)}) fusion(bf16[4,4,4,8,128]{4,3,2,1,0:T(8,128)(2,1)S(1)} %reshape.73, bf16[4,256,4,128,1]{3,2,1,0,4:T(4,128)(2,1)} %bitcast.43, pred[4,256]{1,0:T(4,128)(4,1)S(1)} %broadcast_compare_fusion), kind=kOutput, calls=%fused_computation.40 | convolution fusion | flops 33947136 | bytes 1707008 | tf_op jit(solution)/shard_map/bsgjd,bpgd->bsgjp/dot_general | solution.py:21
  11.0 0.0 copy-done.4
  11.0 0.7 fusion.24
  11.7 12.9 %pmax.7 = f32[4,4,4,8]{3,1,2,0:T(4,128)S(1)} all-reduce(f32[4,4,4,8]{3,1,2,0:T(4,128)S(1)} %max.5), channel_id=1, replica_groups=mesh['rep'=8,'tp'=4] {'tp'}, use_global_device_ids=true, to_apply=%region_2.3 | all-reduce | flops 512 | bytes 4096 | tf_op jit(solution)/shard_map/pmax | solution.py:34
  24.7 0.0 copy-start.5
  24.7 1.5 %fusion.6 = f32[4,4,4,8,128]{4,3,2,1,0:T(8,128)S(1)} fusion(bf16[4,256,4,128,1]{3,2,1,0,4:T(4,128)(2,1)} %bitcast.33, f32[4,4,4,8,256]{4,3,1,2,0:T(8,128)S(1)} %get-tuple-element.5, f32[4,4,4,8]{3,1,2,0:T(4,128)S(1)} %pmax.7), kind=kOutput, calls=%fused_computation.10 | convolution fusion | flops 33816576 | bytes 1837056 | tf_op jit(solution)/shard_map/bsgjp,bpgd->bsgjd/dot_general | solution.py:38
  26.2 0.0 copy-done.2
  26.2 0.3 fusion.3
  26.5 0.1 copy.84
  26.6 0.7 reshape.82
  27.3 0.0 reduce-scatter.8.cloned.1.call-update
  27.3 0.0 reduce-scatter.6.cloned.1.call-start
  27.4 0.3 fusion.9
  27.7 0.1 fusion.15
  27.9 0.1 convert_element_type.62
  27.9 0.0 copy-done.5
  27.9 0.6 dynamic-slice
  29.2 5.8 %all-reduce = bf16[4,4,32]{2,1,0:T(4,128)(2,1)S(1)} all-reduce(bf16[4,4,32]{2,1,0:T(4,128)(2,1)S(1)} %convert_element_type.62), channel_id=3, replica_groups=mesh['rep'=8,'tp'=4] {'tp'}, use_global_device_ids=true, to_apply=%region_6.7.clone | all-reduce | flops 512 | bytes 2048
  35.0 0.1 dynamic-slice_convert_fusion
  35.0 12.4 %reduce-scatter.8.cloned.1.call-done = bf16[8,2048]{1,0:T(8,128)(2,1)} async-done(((bf16[32,2048]{1,0:T(8,128)(2,1)}), bf16[8,2048]{1,0:T(8,128)(2,1)}) %reduce-scatter.8.cloned.1.call-update) | async-done | bytes 32784
  47.4 0.8 reshape.83
  48.2 0.1 divide_convert_fusion
  48.3 0.0 copy-start.1
  48.3 30.9 %all_gather.3 = bf16[128,1024]{1,0:T(8,128)(2,1)S(1)} all-gather(bf16[16,1024]{1,0:T(8,128)(2,1)S(1)} %bitcast.39), channel_id=1, replica_groups=mesh['rep'=8,'tp'=4] {'rep'}, dimensions={0}, use_global_device_ids=true | all-gather | bytes 294912 | tf_op jit(solution)/shard_map/all_gather | solution.py:63
  79.2 0.0 copy-done
  79.2 0.0 copy-start.3
  79.2 0.4 convolution_convert_fusion
  79.7 13.5 %all_to_all.19 = bf16[8,16,1024]{2,1,0:T(8,128)(2,1)S(1)} all-to-all(bf16[8,16,1024]{2,1,0:T(8,128)(2,1)S(1)} %bitcast.34), channel_id=1, replica_groups=mesh['rep'=8,'tp'=4] {'rep'}, dimensions={0} | all-to-all | bytes 524288 | tf_op jit(solution)/shard_map/all_to_all | solution.py:67
  93.2 0.7 copy.58
  93.9 0.0 reduce-scatter.6.cloned.1.call-update
  93.9 0.0 copy-done.1
  94.0 0.0 copy-done.3
  94.0 17.5 %reduce-scatter.6.cloned.1.call-done = bf16[16,2048]{1,0:T(8,128)(2,1)} async-done(((bf16[16,8192]{1,0:T(8,128)(2,1)}), bf16[16,2048]{1,0:T(8,128)(2,1)}) %reduce-scatter.6.cloned.1.call-update) | async-done | bytes 65552 | tf_op jit(solution)/shard_map/reduce_scatter | solution.py:70
  111.5 1.0 multiply_reduce_fusion
  112.5 5.8 %psum.7 = f32[16]{0:T(128)S(1)} all-reduce(f32[16]{0:T(128)S(1)} %multiply_reduce_fusion), channel_id=1, replica_groups=mesh['rep'=8,'tp'=4] {'tp'}, use_global_device_ids=true, to_apply=%region_9.10 | all-reduce | flops 16 | bytes 128 | tf_op jit(solution)/shard_map/psum | solution.py:74
  118.3 0.9 multiply_convert_fusion
  119.2 0.7 reshape.75
  119.9 0.7 reshape.76
  (10 shorter events, 0.1 us)
Async XLA Ops:
  7.2 72.1 %copy-start = (bf16[1024,1024]{1,0:T(8,128)(2,1)S(1)}, bf16[1024,1024]{1,0:T(8,128)(2,1)}, u32[]{:S(2)}) copy-start(bf16[1024,1024]{1,0:T(8,128)(2,1)} %param.16) | copy-start | bytes 6291460
  7.2 3.8 %copy-start.4 = (bf16[4,4,4,128]{3,2,1,0:T(4,128)(2,1)S(1)}, bf16[4,4,4,128]{3,2,1,0:T(4,128)(2,1)}, u32[]{:S(2)}) copy-start(bf16[4,4,4,128]{3,2,1,0:T(4,128)(2,1)} %param.11) | copy-start | bytes 49156
  7.2 40.2 %reduce-scatter.8.cloned.1.call-start = ((), (), s32[]{:S(2)}) async-start(), calls=%async_computation.4 | async-start | bytes 163840
  9.2 17.0 %copy-start.2 = (bf16[4,4,4,128]{3,2,1,0:T(4,128)(2,1)S(1)}, bf16[4,4,4,128]{3,2,1,0:T(4,128)(2,1)}, u32[]{:S(2)}) copy-start(bf16[4,4,4,128]{3,2,1,0:T(4,128)(2,1)} %param.12) | copy-start | bytes 49156
  24.7 3.3 %copy-start.5 = (u32[32]{0:T(128)S(1)}, u32[32]{0:T(128)}, u32[]{:S(2)}) copy-start(u32[32]{0:T(128)} %constant.31) | copy-start | bytes 388
  27.3 84.2 %reduce-scatter.6.cloned.1.call-start = ((), (), s32[]{:S(2)}) async-start(), calls=%async_computation.3 | async-start | bytes 327680 | tf_op jit(solution)/shard_map/reduce_scatter | solution.py:70
  48.3 45.6 %copy-start.1 = (bf16[4,4,2048]{2,1,0:T(4,128)(2,1)S(1)}, bf16[4,4,2048]{2,1,0:T(4,128)(2,1)}, u32[]{:S(2)}) copy-start(bf16[4,4,2048]{2,1,0:T(4,128)(2,1)} %param.9) | copy-start | bytes 196612
  79.2 14.7 %copy-start.3 = (bf16[2048]{0:T(1024)(128)(2,1)S(1)}, bf16[2048]{0:T(1024)(128)(2,1)}, u32[]{:S(2)}) copy-start(bf16[2048]{0:T(1024)(128)(2,1)} %param.17) | copy-start | bytes 12292
Sparse Core Ops, SparseCore 0:
  27.4 19.9 reduce-scatter.7
  94.1 17.4 reduce-scatter.5
where the time goes:
time: 128 us; the launch traced here: 127 us
  blocking collectives  68.9 us (54%)
  waiting for transfers between devices  29.9 us (23%)
  between operations  14.9 us (12%)
  local copies, waits for them, and re-layouts  5.54 us (4%)
  matrix products  4.72 us (4%)
  other arithmetic  3.27 us (3%)
    all_gather x1, blocking collectives, on_device(): lax.all_gather(attended, 'rep', axis=0, tiled=True)  30.9 us
    reduce_scatter x1, waiting for transfers between devices, on_device(): lax.psum_scatter(partial_value.astype(jnp.bfloat16), 'tp', scatter_dimens...  17.5 us
    all_to_all x1, blocking collectives, on_device(): lax.all_to_all(projected, 'rep', split_axis=0, concat_axis=1, tiled=True)  13.5 us
    pmax x1, blocking collectives, on_device(): maxima = lax.pmax(local_maxima, 'tp')  12.9 us
    unnamed x3, waiting for transfers between devices  12.4 us
    unnamed x1, blocking collectives  5.77 us
    psum x1, blocking collectives, on_device(): squares = lax.psum(jnp.sum(hidden * hidden, axis=1), 'tp')  5.76 us
  transfers between devices with their start and end apart: 2, of which 2 were waited for; matrix products, arithmetic and copies ran while one was open for 1% of the time, Pallas kernels for 0%

commit v1 on v0

--- a/solution.py
+++ b/solution.py
@@ -1,10 +1,20 @@
+import functools
 import math
 import jax
 import jax.numpy as jnp
 from jax import lax
 from jax.sharding import PartitionSpec as P
+from jax.lax import all_to_all, psum
 
 D = 8192
+
+
+def rings_start(view, pos_dim, bus_axis):
+    piece_next = all_to_all(jnp.stack(psum(1, bus_axis) * [view], 0), bus_axis, 0, 0)
+    return jnp.concatenate(piece_next, pos_dim)
+
+
+spot_launch = functools.partial(rings_start, pos_dim=0, bus_axis="rep")
 
 
 def on_device(
@@ -60,9 +70,7 @@
     attended = (numerator / denominator[..., None]).astype(jnp.bfloat16)
     attended = attended.reshape(row_count * step_count, -1)
     projected = jnp.dot(
-        lax.all_gather(attended, "rep", axis=0, tiled=True),
-        out_weight,
-        preferred_element_type=jnp.float32,
+        spot_launch(attended), out_weight, preferred_element_type=jnp.float32
     ).astype(jnp.bfloat16)
     partial_value = lax.all_to_all(
         projected, "rep", split_axis=0, concat_axis=1, tiled=True

time: 128 us -> 110 us (0.86)
  blocking collectives: 68.9 us -> 50 us
    all_gather x1 -> x0, blocking collectives: 30.9 us -> none  [on_device(): lax.all_gather(attended, 'rep', axis=0, tiled=True)]
    all_to_all x0 -> x1, blocking collectives: none -> 13.8 us  [rings_start(): all_to_all(jnp.stack(psum(1, bus_axis) * [view], 0), bus_axis, 0, 0)]
    all_to_all x1, blocking collectives: 13.5 us -> 11.8 us  [on_device(): lax.all_to_all(projected, 'rep', split_axis=0, concat_axis=1, tiled=True)]
where the time goes in v1:
time: 110 us; the launch traced here: 109 us
  blocking collectives  50 us (45%)
  waiting for transfers between devices  30.6 us (28%)
  between operations  14.9 us (14%)
  local copies, waits for them, and re-layouts  5.56 us (5%)
  matrix products  4.72 us (4%)
  other arithmetic  3.27 us (3%)
    reduce_scatter x1, waiting for transfers between devices, on_device(): lax.psum_scatter(partial_value.astype(jnp.bfloat16), 'tp', scatter_dimens...  18.2 us
    all_to_all x1, blocking collectives, rings_start(): all_to_all(jnp.stack(psum(1, bus_axis) * [view], 0), bus_axis, 0, 0)  13.8 us
    pmax x1, blocking collectives, on_device(): maxima = lax.pmax(local_maxima, 'tp')  12.9 us
    unnamed x3, waiting for transfers between devices  12.4 us
    all_to_all x1, blocking collectives, on_device(): lax.all_to_all(projected, 'rep', split_axis=0, concat_axis=1, tiled=True)  11.8 us
    unnamed x1, blocking collectives  5.77 us
    psum x1, blocking collectives, on_device(): squares = lax.psum(jnp.sum(hidden * hidden, axis=1), 'tp')  5.76 us
  transfers between devices with their start and end apart: 2, of which 2 were waited for; matrix products, arithmetic and copies ran while one was open for 1% of the time, Pallas kernels for 0%

profile of v1, /device:TPU:0, one launch (start us, length us, event | category | flops | bytes accessed | tf_op | source)
XLA Modules:
  0.0 109.2 jit_solution(9250707256580217124)
XLA Ops:
  7.2 0.0 copy-start
  7.2 0.0 copy-start.4
  7.2 0.0 reduce-scatter.8.cloned.1.call-start
  7.2 1.2 %reshape.75 = bf16[4,4,4,8,128]{4,3,2,1,0:T(8,128)(2,1)S(1)} reshape(bf16[4,4,4096]{2,1,0:T(4,128)(2,1)} %param.10) | data formatting | bytes 262144 | tf_op jit(solution)/shard_map/reshape | solution.py:29
  8.5 0.7 broadcast_compare_fusion
  9.2 0.0 copy-start.2
  9.2 1.8 %fusion.23 = (f32[4,4,4,8]{3,1,2,0:T(4,128)S(1)}, f32[4,4,4,8,256]{4,3,1,2,0:T(8,128)S(1)}) fusion(bf16[4,4,4,8,128]{4,3,2,1,0:T(8,128)(2,1)S(1)} %reshape.75, bf16[4,256,4,128,1]{3,2,1,0,4:T(4,128)(2,1)} %bitcast.45, pred[4,256]{1,0:T(4,128)(4,1)S(1)} %broadcast_compare_fusion), kind=kOutput, calls=%fused_computation.40 | convolution fusion | flops 33947136 | bytes 1707008 | tf_op jit(solution)/shard_map/bsgjd,bpgd->bsgjp/dot_general | solution.py:31
  11.0 0.0 copy-done.4
  11.0 0.7 fusion.24
  11.7 12.9 %pmax.7 = f32[4,4,4,8]{3,1,2,0:T(4,128)S(1)} all-reduce(f32[4,4,4,8]{3,1,2,0:T(4,128)S(1)} %max.5), channel_id=1, replica_groups=mesh['rep'=8,'tp'=4] {'tp'}, use_global_device_ids=true, to_apply=%region_2.3 | all-reduce | flops 512 | bytes 4096 | tf_op jit(solution)/shard_map/pmax | solution.py:44
  24.7 0.0 copy-start.5
  24.7 1.5 %fusion.6 = f32[4,4,4,8,128]{4,3,2,1,0:T(8,128)S(1)} fusion(bf16[4,256,4,128,1]{3,2,1,0,4:T(4,128)(2,1)} %bitcast.34, f32[4,4,4,8,256]{4,3,1,2,0:T(8,128)S(1)} %get-tuple-element.5, f32[4,4,4,8]{3,1,2,0:T(4,128)S(1)} %pmax.7), kind=kOutput, calls=%fused_computation.10 | convolution fusion | flops 33816576 | bytes 1837056 | tf_op jit(solution)/shard_map/bsgjp,bpgd->bsgjd/dot_general | solution.py:48
  26.2 0.0 copy-done.2
  26.2 0.3 fusion.3
  26.5 0.1 copy.84
  26.6 0.7 reshape.84
  27.3 0.0 reduce-scatter.8.cloned.1.call-update
  27.3 0.0 reduce-scatter.6.cloned.1.call-start
  27.4 0.3 fusion.9
  27.7 0.1 fusion.15
  27.9 0.1 convert_element_type.62
  27.9 0.0 copy-done.5
  27.9 0.6 dynamic-slice
  29.2 5.8 %all-reduce = bf16[4,4,32]{2,1,0:T(4,128)(2,1)S(1)} all-reduce(bf16[4,4,32]{2,1,0:T(4,128)(2,1)S(1)} %convert_element_type.62), channel_id=3, replica_groups=mesh['rep'=8,'tp'=4] {'tp'}, use_global_device_ids=true, to_apply=%region_6.7.clone | all-reduce | flops 512 | bytes 2048
  35.0 0.1 dynamic-slice_convert_fusion
  35.0 12.4 %reduce-scatter.8.cloned.1.call-done = bf16[8,2048]{1,0:T(8,128)(2,1)} async-done(((bf16[32,2048]{1,0:T(8,128)(2,1)}), bf16[8,2048]{1,0:T(8,128)(2,1)}) %reduce-scatter.8.cloned.1.call-update) | async-done | bytes 32784
  47.4 0.8 reshape.85
  48.2 0.1 divide_convert_fusion
  48.3 13.8 %all_to_all.24 = bf16[8,16,1024]{2,1,0:T(8,128)(2,1)S(1)} all-to-all(bf16[8,16,1024]{2,1,0:T(8,128)(2,1)S(1)} %stack.3), channel_id=1, replica_groups=mesh['rep'=8,'tp'=4] {'rep'}, dimensions={0} | all-to-all | bytes 524288 | tf_op jit(solution)/shard_map/all_to_all | solution.py:13
  62.1 0.0 copy-start.1
  62.1 0.0 copy-start.3
  62.1 0.0 copy-done
  62.1 0.4 convolution_convert_fusion
  62.6 11.8 %all_to_all.25 = bf16[8,16,1024]{2,1,0:T(8,128)(2,1)S(1)} all-to-all(bf16[8,16,1024]{2,1,0:T(8,128)(2,1)S(1)} %bitcast.36), channel_id=1, replica_groups=mesh['rep'=8,'tp'=4] {'rep'}, dimensions={0} | all-to-all | bytes 524288 | tf_op jit(solution)/shard_map/all_to_all | solution.py:75
  74.4 0.7 copy.58
  75.1 0.0 reduce-scatter.6.cloned.1.call-update
  75.1 0.0 copy-done.1
  75.1 0.0 copy-done.3
  75.2 18.2 %reduce-scatter.6.cloned.1.call-done = bf16[16,2048]{1,0:T(8,128)(2,1)} async-done(((bf16[16,8192]{1,0:T(8,128)(2,1)}), bf16[16,2048]{1,0:T(8,128)(2,1)}) %reduce-scatter.6.cloned.1.call-update) | async-done | bytes 65552 | tf_op jit(solution)/shard_map/reduce_scatter | solution.py:78
  93.3 1.0 multiply_reduce_fusion
  94.3 5.8 %psum.7 = f32[16]{0:T(128)S(1)} all-reduce(f32[16]{0:T(128)S(1)} %multiply_reduce_fusion), channel_id=1, replica_groups=mesh['rep'=8,'tp'=4] {'tp'}, use_global_device_ids=true, to_apply=%region_9.10 | all-reduce | flops 16 | bytes 128 | tf_op jit(solution)/shard_map/psum | solution.py:82
  100.1 0.9 multiply_convert_fusion
  101.0 0.7 reshape.77
  101.7 0.7 reshape.78
  (11 shorter events, 0.1 us)
Async XLA Ops:
  7.2 55.0 %copy-start = (bf16[1024,1024]{1,0:T(8,128)(2,1)S(1)}, bf16[1024,1024]{1,0:T(8,128)(2,1)}, u32[]{:S(2)}) copy-start(bf16[1024,1024]{1,0:T(8,128)(2,1)} %param.16) | copy-start | bytes 6291460
  7.2 3.8 %copy-start.4 = (bf16[4,4,4,128]{3,2,1,0:T(4,128)(2,1)S(1)}, bf16[4,4,4,128]{3,2,1,0:T(4,128)(2,1)}, u32[]{:S(2)}) copy-start(bf16[4,4,4,128]{3,2,1,0:T(4,128)(2,1)} %param.11) | copy-start | bytes 49156
  7.2 40.2 %reduce-scatter.8.cloned.1.call-start = ((), (), s32[]{:S(2)}) async-start(), calls=%async_computation.5 | async-start | bytes 163840
  9.2 17.0 %copy-start.2 = (bf16[4,4,4,128]{3,2,1,0:T(4,128)(2,1)S(1)}, bf16[4,4,4,128]{3,2,1,0:T(4,128)(2,1)}, u32[]{:S(2)}) copy-start(bf16[4,4,4,128]{3,2,1,0:T(4,128)(2,1)} %param.12) | copy-start | bytes 49156
  24.7 3.3 %copy-start.5 = (u32[32]{0:T(128)S(1)}, u32[32]{0:T(128)}, u32[]{:S(2)}) copy-start(u32[32]{0:T(128)} %constant.31) | copy-start | bytes 388
  27.3 66.0 %reduce-scatter.6.cloned.1.call-start = ((), (), s32[]{:S(2)}) async-start(), calls=%async_computation.4 | async-start | bytes 327680 | tf_op jit(solution)/shard_map/reduce_scatter | solution.py:78
  62.1 13.0 %copy-start.1 = (bf16[4,4,2048]{2,1,0:T(4,128)(2,1)S(1)}, bf16[4,4,2048]{2,1,0:T(4,128)(2,1)}, u32[]{:S(2)}) copy-start(bf16[4,4,2048]{2,1,0:T(4,128)(2,1)} %param.9) | copy-start | bytes 196612
  62.1 13.0 %copy-start.3 = (bf16[2048]{0:T(1024)(128)(2,1)S(1)}, bf16[2048]{0:T(1024)(128)(2,1)}, u32[]{:S(2)}) copy-start(bf16[2048]{0:T(1024)(128)(2,1)} %param.17) | copy-start | bytes 12292
Sparse Core Ops, SparseCore 0:
  27.4 19.9 reduce-scatter.7
  75.2 18.0 reduce-scatter.5
